TPU v7x, 256 devices: a whole 4x4x8 slice. The times are simulated.
256 devices in a mesh: gx: 4 (over z_lo), gy: 8 (over x, z_hi), gz: 8 (over y, core).
Axes of the slice: x: 4, y: 4, z: 8 (z_hi: 2, z_lo: 4; z = z_hi * 4 + z_lo), core: 2. Of those that a mesh axis runs over, the one named last changes fastest.
Arguments:
- attn_out: bfloat16 [16384, 8192], P('gx', ('gy', 'gz')), may hold values from -16 to 16
- out_grad: bfloat16 [16384, 8192], P('gx', ('gz', 'gy')), may hold values from -0.046875 to 0.046875
- valid_counts: int32 [16], P('gx'), may hold values from 128 to 1024
Outputs:
- weight_grad: float32 [8192, 8192], P(('gy', 'gx'), 'gz')
Inputs may be any that keep to these rules, and one draw needn't show every extreme that they name: `valid_counts`: valid tokens of a packed row come first, padding after.
All inputs are finite; a program needn't handle non-finite values.
Results may differ from a plain program's by a relative error of at most 0.0003.
Values may be sent and summed in bfloat16 or wider, within the bound.
A program may use at most 64 MiB of HBM per device.

v0:
```python
import jax
import jax.numpy as jnp
from jax import lax
from jax.sharding import Mesh
from jax.sharding import PartitionSpec as P

GY = ("gy_0", "gy_1")
GY_GZ = ("gy_0", "gy_1", "gz")
GZ_GY = ("gz", "gy_0", "gy_1")
GY_GX = ("gy_0", "gy_1", "gx")


def whole_of(value, axes, dim):
    out = value
    for number in range(len(axes) - 1, -1, -1):
        out = lax.all_gather(out, axes[number], axis=dim, tiled=True)
    return out


def split_up(value, dim, peers):
    lengths = value.shape
    tiles = value.reshape(*lengths[:dim], peers, lengths[dim] // peers, *lengths[dim + 1 :])
    return jnp.moveaxis(tiles, dim, 0)


def summed_on_arrival(value, axis, dim):
    tiles = split_up(value, dim, lax.axis_size(axis))
    arrived = lax.all_to_all(tiles, axis, split_axis=0, concat_axis=0, tiled=True)
    return arrived.sum(axis=0)


def transpose_product(inputs, grads):
    return lax.dot_general(
        inputs, grads, (((0,), (0,)), ((), ())), preferred_element_type=jnp.float32
    )


def shards(attn_out, out_grad, valid_counts):
    rows_here = valid_counts.shape[0]
    slot_count = attn_out.shape[0] // rows_here
    positions = lax.broadcasted_iota(jnp.int32, (rows_here, slot_count), 1)
    kept_rows = (positions < valid_counts[:, None]).reshape(-1)
    gathered_inputs = lax.all_gather(attn_out, "gz", axis=1, tiled=True)
    gathered_grads = whole_of(out_grad, GY, 1)
    masked = jnp.where(kept_rows[:, None], gathered_grads, jnp.zeros((), gathered_grads.dtype))
    partial_grad = transpose_product(gathered_inputs, masked)
    return summed_on_arrival(partial_grad, "gx", 0)


def solution(mesh):
    split = Mesh(
        mesh.devices.reshape(mesh.shape["gx"], 4, 2, mesh.shape["gz"]), ("gx", "gy_0", "gy_1", "gz")
    )
    return jax.shard_map(
        shards,
        mesh=split,
        in_specs=(P("gx", GY_GZ), P("gx", GZ_GY), P("gx")),
        out_specs=P(GY_GX, "gz"),
        check_vma=False,
    )
```

profile of v0, /device:TPU:8, one launch (start us, length us, event | category | flops | bytes accessed | tf_op | source)
XLA Modules:
  0.0 345.3 jit_solution(17290514149555261762)
XLA Ops:
  6.5 0.0 all-gather.4.cloned.1.call-start
  6.5 0.7 all-gather.4.cloned.1.call-update
  7.3 0.0 all-gather.8.cloned.1.call-start
  7.3 0.7 all-gather.8.cloned.1.call-update
  8.0 0.0 all-gather.6.cloned.1.call-start
  8.1 69.1 %all-gather.4.cloned.1.call-done = bf16[4096,256]{1,0:T(8,128)(2,1)} async-done(((bf16[4096,128]{1,0:T(8,128)(2,1)}), bf16[4096,256]{1,0:T(8,128)(2,1)}) %all-gather.4.cloned.1.call-update) | async-done | bytes 2097168 | tf_op jit(solution)/shard_map/all_gather | solution.py:16
  77.1 0.0 all-gather.6.cloned.1.call-update
  77.2 0.7 fusion.4
  77.9 53.2 %all-gather.8.cloned.1.call-done = bf16[4096,1024]{1,0:T(8,128)(2,1)} async-done(((bf16[4096,128]{1,0:T(8,128)(2,1)}), bf16[4096,1024]{1,0:T(8,128)(2,1)}) %all-gather.8.cloned.1.call-update) | async-done | bytes 8388624 | tf_op jit(solution)/shard_map/all_gather | solution.py:43
  131.1 92.2 %all-gather.6.cloned.1.call-done = bf16[4096,1024]{1,0:T(8,128)(2,1)} async-done(((bf16[4096,256]{1,0:T(8,128)(2,1)}), bf16[4096,1024]{1,0:T(8,128)(2,1)}) %all-gather.6.cloned.1.call-update) | async-done | bytes 8388624 | tf_op jit(solution)/shard_map/all_gather | solution.py:16
  223.3 15.3 %fusion = f32[1024,1024]{0,1:T(8,128)S(1)} fusion(bf16[4096,1024]{1,0:T(8,128)(2,1)} %all-gather.8.cloned.1.call-done, bf16[4096,1024]{1,0:T(8,128)(2,1)} %all-gather.6.cloned.1.call-done, pred[4096]{0:T(1024)(128)(4,1)S(1)} %bitcast.10), kind=kOutput, calls=%fused_computation | convolution fusion | flops 8594128896 | bytes 20975616 | tf_op jit(solution)/shard_map/dot_general | solution.py:33
  238.6 96.5 %all_to_all.5 = f32[4,256,1024]{2,1,0:T(8,128)} all-to-all(f32[4,256,1024]{2,1,0:T(8,128)S(1)} %bitcast.9), channel_id=1, replica_groups=mesh['gx'=4,'gy_0'=4,'gy_1'=2,'gz'=8] {'gx'}, dimensions={0} | all-to-all | bytes 8388608 | tf_op jit(solution)/shard_map/all_to_all | solution.py:28
  335.1 3.7 %reduce_sum.9 = f32[256,1024]{1,0:T(8,128)} reduce(f32[4,256,1024]{2,1,0:T(8,128)} %all_to_all.5, f32[]{:T(128)} %constant.1.clone.1), dimensions={0}, to_apply=%region_0.1 | reduce | flops 786432 | bytes 5242884 | tf_op jit(solution)/shard_map/reduce_sum | solution.py:29
  (1 shorter events, 0.0 us)
Async XLA Ops:
  6.5 70.6 %all-gather.4.cloned.1.call-start = ((), (), s32[]{:S(2)}) async-start(), calls=%async_computation.1 | async-start | bytes 3145728 | tf_op jit(solution)/shard_map/all_gather | solution.py:16
  7.3 123.8 %all-gather.8.cloned.1.call-start = ((), (), s32[]{:S(2)}) async-start(), calls=%async_computation.3 | async-start | bytes 9437184 | tf_op jit(solution)/shard_map/all_gather | solution.py:43
  8.0 215.3 %all-gather.6.cloned.1.call-start = ((), (), s32[]{:S(2)}) async-start(), calls=%async_computation.2 | async-start | bytes 10485760 | tf_op jit(solution)/shard_map/all_gather | solution.py:16
Sparse Core Ops, SparseCore 0:
  9.1 67.9 all-gather.3
  79.0 52.0 all-gather.7
  132.9 90.3 all-gather.5
where the time goes:
time: 345 us
  waiting for transfers between devices  216 us (63%)
  blocking collectives  96.5 us (28%)
  matrix products  15.3 us (4%)
  between operations  13.1 us (4%)
  other arithmetic  4.42 us (1%)
    all_gather x2, waiting for transfers between devices, whole_of(): out = lax.all_gather(out, axes[number], axis=dim, tiled=True)  161 us
    all_to_all x1, blocking collectives, summed_on_arrival(): lax.all_to_all(tiles, axis, split_axis=0, concat_axis=0, tiled=True)  96.5 us
    all_gather x1, waiting for transfers between devices, shards(): gathered_inputs = lax.all_gather(attn_out, 'gz', axis=1, tiled=True)  53.2 us
    dot_general x1, matrix products, transpose_product(): lax.dot_general(inputs, grads, (((0,), (0,)), ((), ())), preferred_elemen...  15.3 us
  transfers between devices with their start and end apart: 3, of which 3 were waited for; matrix products, arithmetic and copies ran while one was open for 0% of the time, Pallas kernels for 0%

commit v1 on v0

--- a/solution.py
+++ b/solution.py
@@ -8,6 +8,27 @@
 GY_GZ = ("gy_0", "gy_1", "gz")
 GZ_GY = ("gz", "gy_0", "gy_1")
 GY_GX = ("gy_0", "gy_1", "gx")
+
+
+def ring_gather(value, axis, dim):
+    devices, index, width = (lax.axis_size(axis), lax.axis_index(axis), value.shape[dim])
+    right = [(i, (i + 1) % devices) for i in range(devices)]
+    left = [(i, (i - 1) % devices) for i in range(devices)]
+    out = jnp.zeros((*value.shape[:dim], devices * width, *value.shape[dim + 1 :]), value.dtype)
+    out = lax.dynamic_update_slice_in_dim(out, value, index * width, axis=dim)
+    from_left = from_right = value
+    half = devices // 2
+    for hop in range(1, half + 1):
+        from_left = lax.ppermute(from_left, axis, right)
+        out = lax.dynamic_update_slice_in_dim(
+            out, from_left, (index - hop) % devices * width, axis=dim
+        )
+        if hop < devices - half:
+            from_right = lax.ppermute(from_right, axis, left)
+            out = lax.dynamic_update_slice_in_dim(
+                out, from_right, (index + hop) % devices * width, axis=dim
+            )
+    return out
 
 
 def whole_of(value, axes, dim):
@@ -40,7 +61,7 @@
     slot_count = attn_out.shape[0] // rows_here
     positions = lax.broadcasted_iota(jnp.int32, (rows_here, slot_count), 1)
     kept_rows = (positions < valid_counts[:, None]).reshape(-1)
-    gathered_inputs = lax.all_gather(attn_out, "gz", axis=1, tiled=True)
+    gathered_inputs = ring_gather(attn_out, "gz", 1)
     gathered_grads = whole_of(out_grad, GY, 1)
     masked = jnp.where(kept_rows[:, None], gathered_grads, jnp.zeros((), gathered_grads.dtype))
     partial_grad = transpose_product(gathered_inputs, masked)

time: 345 us -> 286 us (0.83)
  waiting for transfers between devices: 216 us -> 137 us
  local copies, waits for them, and re-layouts: 0.01 us -> 14.6 us
  starting transfers between devices: 0.08 us -> 5.92 us
    all_gather x2, waiting for transfers between devices: 161 us -> 98.6 us  [whole_of(): out = lax.all_gather(out, axes[number], axis=dim, tiled=True)]
    all_gather x1 -> x0, waiting for transfers between devices: 53.2 us -> none  [shards(): gathered_inputs = lax.all_gather(attn_out, 'gz', axis=1, tiled=True)]
    ppermute x0 -> x7, waiting for transfers between devices: none -> 37.9 us  [the longest x4 33 us: ring_gather(): from_left = lax.ppermute(from_left, axis, right)]
    dynamic_update_slice x0 -> x8, local copies, waits for them, and re-layouts: none -> 10.3 us  [the longest x4 5.83 us: ring_gather(): lax.dynamic_update_slice_in_dim(out, from_left, (index - hop) % devices *...]
    ppermute x0 -> x7, starting transfers between devices: none -> 5.88 us  [the longest x3 5.86 us: ring_gather(): from_right = lax.ppermute(from_right, axis, left)]
    broadcast_in_dim x0 -> x1, local copies, waits for them, and re-layouts: none -> 4.31 us  [ring_gather(): jnp.zeros((*value.shape[:dim], devices * width, *value.shape[dim + 1:]),...]
  transfers between devices with their start and end apart: 3 -> 9, of which waited for: 3 -> 8; matrix products, arithmetic and copies ran while one was open for 0% -> 5% of each run, Pallas kernels for 0% -> 0%
where the time goes in v1:
time: 286 us
  waiting for transfers between devices  137 us (48%)
  blocking collectives  96.5 us (34%)
  matrix products  14.8 us (5%)
  local copies, waits for them, and re-layouts  14.6 us (5%)
  between operations  13.5 us (5%)
  starting transfers between devices  5.92 us (2%)
  other arithmetic  3.76 us (1%)
    all_gather x2, waiting for transfers between devices, whole_of(): out = lax.all_gather(out, axes[number], axis=dim, tiled=True)  98.6 us
    all_to_all x1, blocking collectives, summed_on_arrival(): lax.all_to_all(tiles, axis, split_axis=0, concat_axis=0, tiled=True)  96.5 us
    ppermute x4, waiting for transfers between devices, ring_gather(): from_left = lax.ppermute(from_left, axis, right)  33 us
    dot_general x1, matrix products, transpose_product(): lax.dot_general(inputs, grads, (((0,), (0,)), ((), ())), preferred_elemen...  14.8 us
    ppermute x3, starting transfers between devices, ring_gather(): from_right = lax.ppermute(from_right, axis, left)  5.86 us
    dynamic_update_slice x4, local copies, waits for them, and re-layouts, ring_gather(): lax.dynamic_update_slice_in_dim(out, from_left, (index - hop) % devices *...  5.83 us
  transfers between devices with their start and end apart: 9, of which 8 were waited for; matrix products, arithmetic and copies ran while one was open for 5% of the time, Pallas kernels for 0%

profile of v1, /device:TPU:8, one launch (start us, length us, event | category | flops | bytes accessed | tf_op | source)
XLA Modules:
  0.0 286.3 jit_solution(7970154354244863458)
XLA Ops:
  6.5 0.7 all-gather.3.cloned.1.call-update
  7.3 69.8 %all-gather.3.cloned.1.call-done = bf16[4096,256]{1,0:T(8,128)(2,1)} async-done(((bf16[4096,128]{1,0:T(8,128)(2,1)}), bf16[4096,256]{1,0:T(8,128)(2,1)}) %all-gather.3.cloned.1.call-update) | async-done | bytes 2097168 | tf_op jit(solution)/shard_map/all_gather | solution.py:37
  77.2 1.7 collective-permute-start.1
  78.9 12.8 %collective-permute-done = bf16[4096,128]{1,0:T(8,128)(2,1)} collective-permute-done((bf16[4096,128]{1,0:T(8,128)(2,1)}, bf16[4096,128]{1,0:T(8,128)(2,1)}, u32[]{:S(2)}, u32[]{:S(2)}) %collective-permute-start) | collective-permute-done | bytes 1048608 | tf_op jit(solution)/shard_map/ppermute | solution.py:22
  91.7 4.3 %broadcast_in_dim.14 = bf16[4096,1024]{1,0:T(8,128)(2,1)} broadcast(bf16[]{:T(256)} %constant.51.clone.1), dimensions={} | broadcast | bytes 8388610 | tf_op jit(solution)/shard_map/broadcast_in_dim | solution.py:17
  96.0 1.1 constant_dynamic-update-slice_fusion.7
  97.1 1.8 collective-permute-start.3
  99.1 7.0 %collective-permute-done.2 = bf16[4096,128]{1,0:T(8,128)(2,1)S(1)} collective-permute-done((bf16[4096,128]{1,0:T(8,128)(2,1)}, bf16[4096,128]{1,0:T(8,128)(2,1)S(1)}, u32[]{:S(2)}, u32[]{:S(2)}) %collective-permute-start.2) | collective-permute-done | bytes 1048608 | tf_op jit(solution)/shard_map/ppermute | solution.py:22
  106.2 2.4 constant_dynamic-update-slice_fusion.6
  108.6 1.1 constant_dynamic-update-slice_fusion.5
  109.7 1.6 collective-permute-done.3
  111.3 2.3 collective-permute-start.5
  113.6 1.2 constant_dynamic-update-slice_fusion.4
  114.8 5.6 %collective-permute-done.4 = bf16[4096,128]{1,0:T(8,128)(2,1)S(1)} collective-permute-done((bf16[4096,128]{1,0:T(8,128)(2,1)S(1)}, bf16[4096,128]{1,0:T(8,128)(2,1)S(1)}, u32[]{:S(2)}, u32[]{:S(2)}) %collective-permute-start.4) | collective-permute-done | bytes 1048608 | tf_op jit(solution)/shard_map/ppermute | solution.py:22
  120.4 1.1 constant_dynamic-update-slice_fusion.3
  121.5 1.1 constant_dynamic-update-slice_fusion.2
  122.6 3.3 %collective-permute-done.5 = bf16[4096,128]{1,0:T(8,128)(2,1)S(1)} collective-permute-done((bf16[4096,128]{1,0:T(8,128)(2,1)S(1)}, bf16[4096,128]{1,0:T(8,128)(2,1)S(1)}, u32[]{:S(2)}, u32[]{:S(2)}) %collective-permute-start.5) | collective-permute-done | bytes 1048608 | tf_op jit(solution)/shard_map/ppermute | solution.py:27
  125.9 1.1 constant_dynamic-update-slice_fusion.1
  127.0 7.6 %collective-permute-done.6 = bf16[4096,128]{1,0:T(8,128)(2,1)S(1)} collective-permute-done((bf16[4096,128]{1,0:T(8,128)(2,1)S(1)}, bf16[4096,128]{1,0:T(8,128)(2,1)S(1)}, u32[]{:S(2)}, u32[]{:S(2)}) %collective-permute-start.6) | collective-permute-done | bytes 1048608 | tf_op jit(solution)/shard_map/ppermute | solution.py:22
  134.6 1.1 constant_dynamic-update-slice_fusion
  135.7 28.7 %all-gather.5.cloned.1.call-done = bf16[4096,1024]{1,0:T(8,128)(2,1)} async-done(((bf16[4096,256]{1,0:T(8,128)(2,1)}), bf16[4096,1024]{1,0:T(8,128)(2,1)}) %all-gather.5.cloned.1.call-update) | async-done | bytes 8388624 | tf_op jit(solution)/shard_map/all_gather | solution.py:37
  164.5 14.8 %fusion = f32[1024,1024]{1,0:T(8,128)S(1)} fusion(bf16[4096,1024]{1,0:T(8,128)(2,1)} %constant_dynamic-update-slice_fusion, bf16[4096,1024]{1,0:T(8,128)(2,1)} %all-gather.5.cloned.1.call-done, pred[4096]{0:T(1024)(128)(4,1)S(1)} %bitcast.8), kind=kOutput, calls=%fused_computation | convolution fusion | flops 8594128896 | bytes 20975616 | tf_op jit(solution)/shard_map/dot_general | solution.py:54
  179.3 96.5 %all_to_all.5 = f32[4,256,1024]{2,1,0:T(8,128)} all-to-all(f32[4,256,1024]{2,1,0:T(8,128)S(1)} %bitcast.7), channel_id=1, replica_groups=mesh['gx'=4,'gy_0'=4,'gy_1'=2,'gz'=8] {'gx'}, dimensions={0} | all-to-all | bytes 8388608 | tf_op jit(solution)/shard_map/all_to_all | solution.py:49
  275.8 3.7 %reduce_sum.9 = f32[256,1024]{1,0:T(8,128)} reduce(f32[4,256,1024]{2,1,0:T(8,128)} %all_to_all.5, f32[]{:T(128)} %constant.65.clone.1), dimensions={0}, to_apply=%region_0.1 | reduce | flops 786432 | bytes 5242884 | tf_op jit(solution)/shard_map/reduce_sum | solution.py:50
  (14 shorter events, 0.2 us)
Async XLA Ops:
  6.5 89.5 %copy-start = (bf16[4096,128]{1,0:T(8,128)(2,1)S(1)}, bf16[4096,128]{1,0:T(8,128)(2,1)}, u32[]{:S(2)}) copy-start(bf16[4096,128]{1,0:T(8,128)(2,1)} %param.3) | copy-start | bytes 3145732
  6.5 92.4 %copy-start.1 = (s32[4]{0:T(128)S(1)}, s32[4]{0:T(128)}, u32[]{:S(2)}) copy-start(s32[4]{0:T(128)} %param.5) | copy-start | bytes 52
  6.5 70.6 %all-gather.3.cloned.1.call-start = ((), (), s32[]{:S(2)}) async-start(), calls=%async_computation.1 | async-start | bytes 3145728 | tf_op jit(solution)/shard_map/all_gather | solution.py:37
  7.3 157.2 %all-gather.5.cloned.1.call-start = ((), (), s32[]{:S(2)}) async-start(), calls=%async_computation.2 | async-start | bytes 10485760 | tf_op jit(solution)/shard_map/all_gather | solution.py:37
  77.2 14.6 %collective-permute-start = (bf16[4096,128]{1,0:T(8,128)(2,1)}, bf16[4096,128]{1,0:T(8,128)(2,1)}, u32[]{:S(2)}, u32[]{:S(2)}) collective-permute-start(bf16[4096,128]{1,0:T(8,128)(2,1)} %param.3), channel_id=1, source_target_pairs={{0,1},{1,2},{2,3},{3,4},{4,5},{5,6},{6,7},{7,0},{8,9},{9,10},{10,1... | collective-permute-start | bytes 3145736 | tf_op jit(solution)/shard_map/ppermute | solution.py:22
  77.2 19.9 %collective-permute-start.1 = (bf16[4096,128]{1,0:T(8,128)(2,1)}, bf16[4096,128]{1,0:T(8,128)(2,1)S(1)}, u32[]{:S(2)}, u32[]{:S(2)}) collective-permute-start(bf16[4096,128]{1,0:T(8,128)(2,1)} %param.3), channel_id=1, source_target_pairs={{0,7},{1,0},{2,1},{3,2},{4,3},{5,4},{6,5},{7,6},{8,15},{9,8},{10,9... | collective-permute-start | bytes 3145736 | tf_op jit(solution)/shard_map/ppermute | solution.py:27
  91.7 14.4 %collective-permute-start.2 = (bf16[4096,128]{1,0:T(8,128)(2,1)}, bf16[4096,128]{1,0:T(8,128)(2,1)S(1)}, u32[]{:S(2)}, u32[]{:S(2)}) collective-permute-start(bf16[4096,128]{1,0:T(8,128)(2,1)} %collective-permute-done), channel_id=1, source_target_pairs={{0,1},{1,2},{2,3},{3,4},{4,5},{5,6},{6,7},{7,0},{8,9},{9,10},{10,1... | collective-permute-start | bytes 3145736 | tf_op jit(solution)/shard_map/ppermute | solution.py:22
  97.1 14.1 %collective-permute-start.3 = (bf16[4096,128]{1,0:T(8,128)(2,1)S(1)}, bf16[4096,128]{1,0:T(8,128)(2,1)S(1)}, u32[]{:S(2)}, u32[]{:S(2)}) collective-permute-start(bf16[4096,128]{1,0:T(8,128)(2,1)S(1)} %collective-permute-done.1), channel_id=1, source_target_pairs={{0,7},{1,0},{2,1},{3,2},{4,3},{5,4},{6,5},{7,6},{8,15},{9,8},{10,9... | collective-permute-start | bytes 3145736 | tf_op jit(solution)/shard_map/ppermute | solution.py:27
  106.2 14.2 %collective-permute-start.4 = (bf16[4096,128]{1,0:T(8,128)(2,1)S(1)}, bf16[4096,128]{1,0:T(8,128)(2,1)S(1)}, u32[]{:S(2)}, u32[]{:S(2)}) collective-permute-start(bf16[4096,128]{1,0:T(8,128)(2,1)S(1)} %collective-permute-done.2), channel_id=1, source_target_pairs={{0,1},{1,2},{2,3},{3,4},{4,5},{5,6},{6,7},{7,0},{8,9},{9,10},{10,1... | collective-permute-start | bytes 3145736 | tf_op jit(solution)/shard_map/ppermute | solution.py:22
  111.3 14.6 %collective-permute-start.5 = (bf16[4096,128]{1,0:T(8,128)(2,1)S(1)}, bf16[4096,128]{1,0:T(8,128)(2,1)S(1)}, u32[]{:S(2)}, u32[]{:S(2)}) collective-permute-start(bf16[4096,128]{1,0:T(8,128)(2,1)S(1)} %collective-permute-done.3), channel_id=1, source_target_pairs={{0,7},{1,0},{2,1},{3,2},{4,3},{5,4},{6,5},{7,6},{8,15},{9,8},{10,9... | collective-permute-start | bytes 3145736 | tf_op jit(solution)/shard_map/ppermute | solution.py:27
  120.4 14.2 %collective-permute-start.6 = (bf16[4096,128]{1,0:T(8,128)(2,1)S(1)}, bf16[4096,128]{1,0:T(8,128)(2,1)S(1)}, u32[]{:S(2)}, u32[]{:S(2)}) collective-permute-start(bf16[4096,128]{1,0:T(8,128)(2,1)S(1)} %collective-permute-done.4), channel_id=1, source_target_pairs={{0,1},{1,2},{2,3},{3,4},{4,5},{5,6},{6,7},{7,0},{8,9},{9,10},{10,1... | collective-permute-start | bytes 3145736 | tf_op jit(solution)/shard_map/ppermute | solution.py:22
Sparse Core Ops, SparseCore 0:
  9.1 67.9 all-gather.2
  79.0 85.4 all-gather.4
